TPU v7x, 32 devices: a whole 2x2x4 slice. The times are simulated.
32 devices in a mesh: rep: 4 (over y, x), col: 8 (over z, core).
Axes of the slice: x: 2, y: 2, z: 4, core: 2. Of those that a mesh axis runs over, the one named last changes fastest.
Arguments:
- tables: float32 [2, 256, 32768], P(None, 'col', 'rep'), may hold values from -4 to 4
- accumulator: float32 [2, 32768], P(None, 'rep'), may hold values from 0.1 to 20
- replica_grads: bfloat16 [4, 2, 256, 16384], P('rep', None, 'col'), may hold values from -6 to 6
- block_ids: int32 [2, 128], replicated, may hold values from 0 to 255, as said below
Outputs:
- new_tables: float32 [2, 256, 32768], P(None, 'col', 'rep')
- new_accumulator: float32 [2, 32768], P(None, 'rep')
Inputs may be any that keep to these rules, and one draw needn't show every extreme that they name: `block_ids`: the block ids of one table are distinct; each names a block of 128 rows. Splitting the 32768 rows into 4 equal runs, each run holds exactly 32 of a table's touched blocks.
All inputs are finite; a program needn't handle non-finite values.
Results may differ from a plain program's by a relative error of at most 0.0003.
Values sent between devices are 32-bit elements; how exact they have to be, the bound alone decides.
A program may use at most 64 MiB of HBM per device.

v0:
```python
import jax
import jax.numpy as jnp
from jax import lax
from jax.sharding import PartitionSpec as P

DIM = 256
BLOCK = 128


def row_squares(total):
    return lax.psum(jnp.sum(total * total, axis=1), "col")


def body(tables, accumulator, replica_grads, block_ids):
    own_grad = replica_grads[0].astype(jnp.float32)
    ntab, width, local_rows = tables.shape
    local_blocks = local_rows // BLOCK
    offset = lax.axis_index("rep") * local_blocks
    full_blocks = own_grad.shape[2] // BLOCK
    per_owner = full_blocks // lax.axis_size("rep")
    arranged = []
    owned_ids = []
    for table in range(ntab):
        owner = block_ids[table] // local_blocks
        order = jnp.argsort(owner, stable=True)
        grouped = own_grad[table].reshape(width, full_blocks, BLOCK)
        arranged.append(jnp.take(grouped, order, axis=1).reshape(width, full_blocks * BLOCK))
        sorted_ids = jnp.take(block_ids[table], order, axis=0)
        owned_ids.append(
            lax.dynamic_slice_in_dim(sorted_ids, lax.axis_index("rep") * per_owner, per_owner)
        )
    total = lax.psum_scatter(jnp.stack(arranged), "rep", scatter_dimension=2, tiled=True)
    squares = row_squares(total)
    used_ids = jnp.stack(owned_ids)
    slab = total.shape[2]
    nblk = slab // BLOCK
    blocked = tables.reshape(ntab, width, local_blocks, BLOCK)
    acc_blocked = accumulator.reshape(ntab, local_blocks, BLOCK)
    out_tab = []
    out_acc = []
    for table in range(ntab):
        local_ids = used_ids[table] - offset
        inside = (local_ids >= 0) & (local_ids < local_blocks)
        safe_ids = jnp.where(inside, local_ids, 0)
        target = jnp.where(inside, local_ids, local_blocks)
        old_rows = jnp.take(blocked[table], safe_ids, axis=1).reshape(width, slab)
        old_accum = jnp.take(acc_blocked[table], safe_ids, axis=0).reshape(slab)
        fresh = old_accum + squares[table] / DIM
        moved = old_rows - 0.1 * total[table] / (jnp.sqrt(fresh)[None, :] + 1e-08)
        new_blocks = (
            blocked[table].at[:, target].set(moved.reshape(width, nblk, BLOCK), mode="drop")
        )
        new_acc = acc_blocked[table].at[target].set(fresh.reshape(nblk, BLOCK), mode="drop")
        out_tab.append(new_blocks.reshape(width, local_rows))
        out_acc.append(new_acc.reshape(local_rows))
    return (jnp.stack(out_tab), jnp.stack(out_acc))


def solution(mesh):
    return jax.shard_map(
        body,
        mesh=mesh,
        in_specs=(P(None, "col", "rep"), P(None, "rep"), P("rep", None, "col", None), P()),
        out_specs=(P(None, "col", "rep"), P(None, "rep")),
        check_vma=False,
    )
```

profile of v0, /device:TPU:0, one launch (start us, length us, event | category | flops | bytes accessed | tf_op | source)
XLA Modules:
  0.0 150.6 jit_solution(7778629519587096425)
XLA Ops:
  8.7 2.5 %sort.31 = (s32[128]{0:T(128)}, s32[128]{0:T(128)S(1)}) sort(s32[128]{0:T(128)S(1)} %get-tuple-element.32, s32[128]{0:T(128)S(1)} %iota.7), dimensions={0}, to_apply=%region_0.1 | sort | flops 896 | bytes 2048 | tf_op jit(solution)/shard_map/jit(argsort)/sort | solution.py:25
  11.3 1.2 gather_fusion
  12.5 2.5 %sort.32 = (s32[128]{0:T(128)}, s32[128]{0:T(128)S(1)}) sort(s32[128]{0:T(128)S(1)} %get-tuple-element.33, s32[128]{0:T(128)S(1)} %iota.8), dimensions={0}, to_apply=%region_1.0 | sort | flops 896 | bytes 2048 | tf_op jit(solution)/shard_map/jit(argsort)/sort | solution.py:25
  15.1 1.2 gather_fusion.5
  16.3 1.9 %convert_element_type.4 = f32[1,2,32,16384]{3,2,1,0:T(8,128)S(1)} convert(bf16[1,2,32,16384]{3,2,1,0:T(8,128)(2,1)} %param.14) | non-fusion elementwise | flops 1048576 | bytes 6291456 | tf_op jit(solution)/shard_map/convert_element_type | solution.py:15
  18.2 1.6 %slice_bitcast_fusion.1 = (f32[4,8,128,128]{3,1,2,0:T(8,128)S(1)}, f32[4,8,128,128]{3,1,2,0:T(8,128)}) fusion(f32[1,2,32,16384]{3,2,1,0:T(8,128)S(1)} %convert_element_type.4), kind=kLoop, calls=%fused_computation.14 | loop fusion | bytes 8388608
  20.2 2.6 %copy.13 = f32[32,128,128]{2,0,1:T(8,128)} copy(f32[32,128,128]{2,1,0:T(8,128)S(1)} %bitcast.60) | data formatting | bytes 4194304 | tf_op jit(solution)/shard_map/reshape;squeeze | solution.py:26
  22.8 2.3 %gather_fusion.2 = f32[128,32,128]{2,1,0:T(8,128)S(1)} fusion(f32[32,128,128]{2,0,1:T(8,128)} %copy.13, s32[1024]{0:T(1024)S(1)} %pad_clamp_fusion.3), kind=kCustom, calls=%fused_computation.2.clone | custom fusion | bytes 4194816 | tf_op jit(solution)/shard_map/jit(_take)/gather | solution.py:27
  25.3 1.2 copy.14
  26.5 1.5 %stack_reshape.18 = f32[1,32,16384]{2,1,0:T(8,128)} reshape(f32[32,128,128]{2,1,0:T(8,128)S(1)} %copy.14) | data formatting | bytes 4194304 | tf_op jit(solution)/shard_map/stack;reshape | solution.py:32
  28.0 2.0 %copy.26 = f32[4,8,128,128]{3,2,1,0:T(8,128)S(1)} copy(f32[4,8,128,128]{3,1,2,0:T(8,128)} %get-tuple-element.19) | data formatting | bytes 4194304
  30.0 2.5 %copy.15 = f32[32,128,128]{2,0,1:T(8,128)} copy(f32[32,128,128]{2,1,0:T(8,128)S(1)} %bitcast.61) | data formatting | bytes 4194304 | tf_op jit(solution)/shard_map/reshape;squeeze | solution.py:26
  32.5 2.3 %gather_fusion.3 = f32[128,32,128]{2,1,0:T(8,128)S(1)} fusion(f32[32,128,128]{2,0,1:T(8,128)} %copy.15, s32[1024]{0:T(1024)S(1)} %pad_clamp_fusion.1), kind=kCustom, calls=%fused_computation.6.clone | custom fusion | bytes 4194816 | tf_op jit(solution)/shard_map/jit(_take)/gather | solution.py:27
  36.3 1.5 %stack_reshape.19 = f32[1,32,16384]{2,1,0:T(8,128)} reshape(f32[32,128,128]{2,1,0:T(8,128)S(1)} %copy.16) | data formatting | bytes 4194304 | tf_op jit(solution)/shard_map/stack;reshape | solution.py:32
  37.8 4.4 %pad_maximum_fusion = f32[2,32,16384]{2,1,0:T(8,128)} fusion(f32[1,32,16384]{2,1,0:T(8,128)} %stack_reshape.19, f32[1,32,16384]{2,1,0:T(8,128)} %stack_reshape.18), kind=kLoop, calls=%fused_computation.12 | loop fusion | flops 1048576 | bytes 8388608 | tf_op jit(solution)/shard_map/stack | solution.py:32
  42.3 1.7 %slice_bitcast_fusion.3 = (f32[4,8,64,128]{3,1,2,0:T(8,128)S(1)}, f32[4,8,64,128]{3,1,2,0:T(8,128)S(1)}) fusion(f32[2,32,8192]{2,1,0:T(8,128)} %param.12), kind=kLoop, calls=%fused_computation.20 | loop fusion | bytes 4194304
  47.5 1.4 gather_fusion.6
  49.2 48.6 %reduce-scatter.2.cloned.1.call-done = f32[2,32,4096]{2,1,0:T(8,128)} async-done(((f32[2,32,16384]{2,1,0:T(8,128)}), f32[2,32,4096]{2,1,0:T(8,128)}) %reduce-scatter.2.cloned.1.call-update) | async-done | bytes 1048592 | tf_op jit(solution)/shard_map/reduce_scatter | solution.py:32
  97.7 1.4 multiply_reduce_fusion
  99.1 28.4 %psum.7 = f32[2,4096]{1,0:T(2,128)S(1)} all-reduce(f32[2,4096]{1,0:T(2,128)S(1)} %multiply_reduce_fusion), channel_id=1, replica_groups=mesh['rep'=4,'col'=8] {'col'}, use_global_device_ids=true, to_apply=%region_4.9 | all-reduce | flops 8192 | bytes 65536 | tf_op jit(solution)/shard_map/psum | solution.py:11
  127.5 2.1 %fusion.1 = (f32[4,8,32,128]{3,1,2,0:T(8,128)S(1)}, f32[4,8,32,128]{3,1,2,0:T(8,128)}) fusion(f32[2,32,4096]{2,1,0:T(8,128)} %reduce-scatter.2.cloned.1.call-done), kind=kLoop, calls=%fused_computation.24 | loop fusion | flops 262144 | bytes 2097152
  131.8 3.4 %scatter_fusion = f32[32,64,128]{2,0,1:T(8,128)S(1)} fusion(f32[32,64,128]{2,0,1:T(8,128)S(1)} %copy.18, s32[32]{0:T(128)S(1)} %get-tuple-element.35, f32[32,32,128]{2,1,0:T(8,128)} %fusion.3), kind=kCustom, calls=%fused_computation.8 | custom fusion | bytes 1572992 | tf_op jit(solution)/shard_map/scatter | solution.py:51
  139.2 1.5 %scatter_fusion.1 = f32[32,64,128]{2,0,1:T(8,128)S(1)} fusion(f32[32,64,128]{2,0,1:T(8,128)S(1)} %copy.22, s32[32]{0:T(128)S(1)} %get-tuple-element.34, f32[32,32,128]{2,1,0:T(8,128)S(1)} %fusion.2), kind=kCustom, calls=%fused_computation.9 | custom fusion | bytes 1572992 | tf_op jit(solution)/shard_map/scatter | solution.py:51
  142.3 1.5 pad_maximum_fusion.1
  (48 shorter events, 15.1 us)
Async XLA Ops:
  7.2 90.6 %reduce-scatter.2.cloned.1.call-start = ((), (), s32[]{:S(2)}) async-start(), calls=%async_computation.1 | async-start | bytes 5242880 | tf_op jit(solution)/shard_map/reduce_scatter | solution.py:32
  44.0 0.9 copy-start.2
  135.7 3.1 %copy-start.1 = (f32[32,32,128]{2,1,0:T(8,128)S(1)}, f32[32,32,128]{2,1,0:T(8,128)}, u32[]{:S(2)}) copy-start(f32[32,32,128]{2,1,0:T(8,128)} %gather_fusion.6) | copy-start | bytes 1572868
  140.7 1.5 %copy-start = (f32[1,32,8192]{2,1,0:T(8,128)S(1)}, f32[1,32,8192]{2,1,0:T(8,128)}, u32[]{:S(2)}) copy-start(f32[1,32,8192]{2,1,0:T(8,128)} %stack_reshape.20) | copy-start | bytes 3145732
Sparse Core Ops, SparseCore 0:
  42.4 55.3 reduce-scatter.1
where the time goes:
time: 151 us
  waiting for transfers between devices  48.6 us (32%)
  local copies, waits for them, and re-layouts  37.5 us (25%)
  blocking collectives  28.4 us (19%)
  other arithmetic  21.7 us (14%)
  between operations  14.3 us (9%)
    reduce_scatter x1, waiting for transfers between devices, body(): lax.psum_scatter(jnp.stack(arranged), 'rep', scatter_dimension=2, tiled=T...  48.6 us
    psum x1, blocking collectives, row_squares(): return lax.psum(jnp.sum(total * total, axis=1), 'col')  28.4 us
    unnamed x14, local copies, waits for them, and re-layouts  7.26 us
    scatter x4, local copies, waits for them, and re-layouts, body(): blocked[table].at[:, target]  6.1 us
    another operation x2, local copies, waits for them, and re-layouts, body(): grouped = own_grad[table].reshape(width, full_blocks, BLOCK)  5.11 us
    sort x2, other arithmetic, body(): order = jnp.argsort(owner, stable=True)  5.07 us
    gather x2, local copies, waits for them, and re-layouts, body(): jnp.take(grouped, order, axis=1).reshape(width, full_blocks * BLOCK)  4.54 us
    another operation x1, other arithmetic, body(): jnp.stack(arranged)  4.45 us
  transfers between devices with their start and end apart: 1, of which 1 were waited for; matrix products, arithmetic and copies ran while one was open for 5% of the time, Pallas kernels for 0%

commit v1 on v0

v1 whole, which is shorter than its diff:
```python
import functools
import math

import jax
import jax.numpy as jnp
from jax import lax
from jax.experimental import pallas as pl
from jax.experimental.pallas import tpu as pltpu
from jax.sharding import PartitionSpec as P

BLOCK = 128
MESH = pl.DeviceIdType.MESH
AHEAD = 2


def layout(mesh, shape, n_slab):
    reps, cols = mesh.shape["rep"], mesh.shape["col"]
    inner = math.isqrt(reps)
    while reps % inner:
        inner -= 1
    ntab, width, _ = shape
    per = n_slab // BLOCK // reps
    group = math.gcd(per, 8)
    return dict(reps=reps, cols=cols, inner=inner, outer=reps // inner, ntab=ntab,
                width=width, per=per, group=group, pieces=per // group)


def pack(cfg, order, grads, packed):
    reps, per, group, pieces = cfg["reps"], cfg["per"], cfg["group"], cfg["pieces"]

    def piece(t, g):
        for owner in range(reps):
            for i in range(group):
                at = order[t, owner * per + g * group + i]
                lanes = pl.ds(pl.multiple_of(at * BLOCK, BLOCK), BLOCK)
                packed[t * pieces + g, owner, :, pl.ds(i * BLOCK, BLOCK)] = grads[0, t, :, lanes].astype(jnp.float32)

    for t in range(cfg["ntab"]):
        lax.fori_loop(0, pieces, lambda g, n, t=t: (piece(t, g), n)[1], 0)


def exchange(cfg, packed, total, squares_out, *scratch):
    reps, cols, inner, outer = cfg["reps"], cfg["cols"], cfg["inner"], cfg["outer"]
    ntab, width, per, group = cfg["ntab"], cfg["width"], cfg["per"], cfg["group"]
    pieces = cfg["pieces"]
    (landed, relayed, landed2, sq_all, s1, r1, s2, r2, s3, r3) = scratch
    chunks = ntab * pieces
    me = lax.axis_index("rep")
    my_col = lax.axis_index("col")
    x, y = lax.rem(me, inner), me // inner

    barrier = pltpu.get_barrier_semaphore()
    for f in range(1, inner):
        pl.semaphore_signal(barrier, inc=1, device_id={"rep": y * inner + lax.rem(x + f, inner)}, device_id_type=MESH)
    for f in range(1, outer):
        pl.semaphore_signal(barrier, inc=1, device_id={"rep": lax.rem(y + f, outer) * inner + x}, device_id_type=MESH)
    for f in range(1, cols):
        pl.semaphore_signal(barrier, inc=1, device_id={"col": lax.rem(my_col + f, cols)}, device_id_type=MESH)

    def axes(c):
        return (inner, outer) if c % 2 == 0 else (outer, inner)

    def rank(c, f, s):
        if c % 2 == 0:
            return lax.rem(y + s, outer) * inner + lax.rem(x + f, inner)
        return lax.rem(y + f, outer) * inner + lax.rem(x + s, inner)

    def place(i):
        return pl.ds(pl.multiple_of(i * BLOCK, BLOCK), BLOCK)

    def own(c, owner, i):
        return packed[c, owner, :, place(i)]

    def each(fn):
        lax.fori_loop(0, group, lambda i, n: (fn(i), n)[1], 0, unroll=True)

    def first_copy(c, f, s):
        return pltpu.make_async_remote_copy(
            packed.at[c, rank(c, f, s)], landed.at[c, f - 1, s], s1.at[c, f - 1, s], r1.at[c, f - 1, s],
            device_id={"rep": rank(c, f, 0)}, device_id_type=MESH)

    def second_copy(c, s):
        return pltpu.make_async_remote_copy(
            relayed.at[c, s - 1], landed2.at[c, s - 1], s2.at[c, s - 1], r2.at[c, s - 1],
            device_id={"rep": rank(c, 0, s)}, device_id_type=MESH)

    def square_copy(c, f):
        return pltpu.make_async_remote_copy(
            sq_all.at[c, my_col], sq_all.at[c, my_col], s3.at[c, f - 1], r3.at[c, f - 1],
            device_id={"col": lax.rem(my_col + f, cols)}, device_id_type=MESH)

    def send(c):
        nf, ns = axes(c)
        for s in [*range(1, ns), 0]:
            for f in range(1, nf):
                first_copy(c, f, s).start()

    def relay(c):
        nf, ns = axes(c)
        for s in range(1, ns):
            for f in range(1, nf):
                first_copy(c, f, s).wait_recv()
            owner = rank(c, 0, s)

            def add(i):
                acc = own(c, owner, i)
                for f in range(1, nf):
                    acc = acc + landed[c, f - 1, s, :, place(i)]
                relayed[c, s - 1, :, place(i)] = acc

            each(add)

    def send_relay(c):
        _, ns = axes(c)
        for s in range(1, ns):
            second_copy(c, s).start()

    def finish(c):
        nf, ns = axes(c)
        for f in range(1, nf):
            first_copy(c, f, 0).wait_recv()
        for s in range(1, ns):
            second_copy(c, s).wait_recv()

        def add(i):
            acc = own(c, me, i)
            for f in range(1, nf):
                acc = acc + landed[c, f - 1, 0, :, place(i)]
            for s in range(1, ns):
                acc = acc + landed2[c, s - 1, :, place(i)]
            total[c, :, place(i)] = acc
            sq_all[c, my_col, pl.ds(i, 1), :] = jnp.sum(acc * acc, axis=0, keepdims=True)

        each(add)

    def send_squares(c):
        for f in range(1, cols):
            square_copy(c, f).start()

    def gather_squares(c):
        for f in range(1, cols):
            square_copy(c, f).wait_recv()
        acc = sq_all[c, 0]
        for f in range(1, cols):
            acc = acc + sq_all[c, f]
        squares_out[c] = acc

    pairs = [[c for c in (k, k + 1) if c < chunks] for k in range(0, chunks, 2)]
    steps = len(pairs)

    def at(k, fns):
        if 0 <= k < steps:
            for fn in fns:
                for c in pairs[k]:
                    fn(c)

    greeted = inner - 1 + outer - 1 + cols - 1
    for k in range(steps + AHEAD + 4):
        if k == 0:
            pl.semaphore_wait(barrier, greeted)
        at(k, [send])
        at(k - AHEAD + 1, [relay, send_relay])
        at(k - AHEAD - 0, [finish, send_squares])
        at(k - AHEAD - 1, [gather_squares])

    for c in range(chunks):
        nf, ns = axes(c)
        for s in range(ns):
            for f in range(1, nf):
                first_copy(c, f, s).wait_send()
        for s in range(1, ns):
            second_copy(c, s).wait_send()
        for f in range(1, cols):
            square_copy(c, f).wait_send()


def update(cfg, dim, ids, total, squares, tables, accumulator, new_tables, new_acc,
           tab, acc, step, out_sem):
    ntab, width, per, group = cfg["ntab"], cfg["width"], cfg["per"], cfg["group"]
    pieces = cfg["pieces"]
    local_blocks = tables.shape[2] // BLOCK
    rows = 8
    parts = width // rows
    me = lax.axis_index("rep")

    def window(ref, t, d):
        return ref.at[t, pl.ds(d * rows, rows)]

    def store(t, d):
        return pltpu.make_async_copy(window(tab, t, d), window(new_tables, t, d), out_sem.at[t, d])

    def target(t, i):
        block = ids[t, me * per + i] - me * local_blocks
        return pl.ds(pl.multiple_of(block * BLOCK, BLOCK), BLOCK)

    new_acc[...] = accumulator[...]
    for t in range(ntab):
        for g in range(pieces):
            c = t * pieces + g
            for i in range(group):
                acc[c, pl.ds(i, 1), :] = accumulator[pl.ds(t, 1), target(t, g * group + i)]
            fresh = acc[c] + squares[c] * (1.0 / dim)
            acc[c] = fresh
            step[c] = 0.1 / (jnp.sqrt(fresh) + 1e-8)
            for i in range(group):
                new_acc[pl.ds(t, 1), target(t, g * group + i)] = acc[c, pl.ds(i, 1), :]
    for t in range(ntab):
        for d in range(parts):
            tab[t, pl.ds(d * rows, rows)] = tables[t, pl.ds(d * rows, rows)]
            for g in range(pieces):
                c = t * pieces + g
                for i in range(group):
                    where = target(t, g * group + i)
                    lanes = pl.ds(i * BLOCK, BLOCK)
                    moved = total[c, pl.ds(d * rows, rows), lanes] * step[c, pl.ds(i, 1), :]
                    tab[t, pl.ds(d * rows, rows), where] = tables[t, pl.ds(d * rows, rows), where] - moved
            store(t, d).start()
    for t in range(ntab):
        for d in range(parts):
            store(t, d).wait()


def body(mesh, tables, accumulator, replica_grads, block_ids):
    cfg = layout(mesh, tables.shape, replica_grads.shape[3])
    ntab, width, per, group = cfg["ntab"], cfg["width"], cfg["per"], cfg["group"]
    cols, pieces = cfg["cols"], cfg["pieces"]
    side = max(cfg["inner"], cfg["outer"])
    chunks, span = ntab * pieces, group * BLOCK
    dim = width * cols
    nslab = replica_grads.shape[3]
    nblk = nslab // BLOCK

    place = jnp.sum((block_ids[:, :, None] > block_ids[:, None, :]).astype(jnp.int32), axis=2)
    hit = place[:, None, :] == jnp.arange(nblk, dtype=jnp.int32)[None, :, None]
    order = jnp.sum(jnp.where(hit, jnp.arange(nblk, dtype=jnp.int32)[None, None, :], 0), axis=2)
    ids = jnp.sum(jnp.where(hit, block_ids[:, None, :], 0), axis=2)

    anyspace = pl.BlockSpec(memory_space=pl.ANY)
    vmem = pl.BlockSpec(memory_space=pltpu.VMEM)
    smem = pl.BlockSpec(memory_space=pltpu.SMEM)
    f32 = jnp.float32
    dma = pltpu.SemaphoreType.DMA
    packed = pl.pallas_call(
        functools.partial(pack, cfg),
        out_shape=jax.ShapeDtypeStruct((chunks, cfg["reps"], width, span), f32),
        in_specs=[smem, vmem],
        out_specs=vmem,
        compiler_params=pltpu.CompilerParams(vmem_limit_bytes=12 * 2**20),
        name="pack",
    )(order, replica_grads)
    total, squares = pl.pallas_call(
        functools.partial(exchange, cfg),
        out_shape=(jax.ShapeDtypeStruct((chunks, width, span), f32),
                   jax.ShapeDtypeStruct((chunks, group, BLOCK), f32)),
        in_specs=[vmem],
        out_specs=(vmem, vmem),
        scratch_shapes=[
            pltpu.VMEM((chunks, side - 1, side, width, span), f32),
            pltpu.VMEM((chunks, side - 1, width, span), f32),
            pltpu.VMEM((chunks, side - 1, width, span), f32),
            pltpu.VMEM((chunks, cols, group, BLOCK), f32),
            dma((chunks, side - 1, side)), dma((chunks, side - 1, side)),
            dma((chunks, side - 1)), dma((chunks, side - 1)),
            dma((chunks, cols - 1)), dma((chunks, cols - 1)),
        ],
        compiler_params=pltpu.CompilerParams(
            collective_id=0, has_side_effects=True, vmem_limit_bytes=24 * 2**20),
        name="exchange",
    )(packed)
    rows = 8
    parts = width // rows
    return pl.pallas_call(
        functools.partial(update, cfg, dim),
        out_shape=(jax.ShapeDtypeStruct(tables.shape, f32),
                   jax.ShapeDtypeStruct(accumulator.shape, f32)),
        in_specs=[smem, vmem, vmem, vmem, vmem],
        out_specs=(anyspace, vmem),
        scratch_shapes=[
            pltpu.VMEM(tables.shape, f32),
            pltpu.VMEM((chunks, group, BLOCK), f32),
            pltpu.VMEM((chunks, group, BLOCK), f32),
            dma((ntab, parts)),
        ],
        compiler_params=pltpu.CompilerParams(vmem_limit_bytes=24 * 2**20),
        name="update",
    )(ids, total, squares, tables, accumulator)


def solution(mesh):
    return jax.shard_map(
        functools.partial(body, mesh),
        mesh=mesh,
        in_specs=(P(None, "col", "rep"), P(None, "rep"), P("rep", None, "col", None), P()),
        out_specs=(P(None, "col", "rep"), P(None, "rep")),
        check_vma=False,
    )
```

time: 151 us -> 54.1 us (0.36)
  Pallas kernels: 0 us -> 49.9 us
  waiting for transfers between devices: 48.6 us -> 0 us
  local copies, waits for them, and re-layouts: 37.5 us -> 1.6 us
  blocking collectives: 28.4 us -> 0 us
  other arithmetic: 21.7 us -> 1.76 us
  between operations: 14.3 us -> 0.69 us
    pallas_call x0 -> x3, Pallas kernels: none -> 49.9 us  [the longest x1 45.7 us: body(): pl.pallas_call(functools.partial(exchange, cfg), out_shape=(jax.ShapeDtyp...]
    reduce_scatter x1 -> x0, waiting for transfers between devices: 48.6 us -> none  [body(): lax.psum_scatter(jnp.stack(arranged), 'rep', scatter_dimension=2, tiled=T...]
    psum x1 -> x0, blocking collectives: 28.4 us -> none  [row_squares(): return lax.psum(jnp.sum(total * total, axis=1), 'col')]
    gather x8 -> x0, local copies, waits for them, and re-layouts: 10.1 us -> none  [the longest x2 4.54 us: body(): jnp.take(grouped, order, axis=1).reshape(width, full_blocks * BLOCK)]
    another operation x6 -> x0, local copies, waits for them, and re-layouts: 9.52 us -> none  [the longest x2 5.11 us: body(): grouped = own_grad[table].reshape(width, full_blocks, BLOCK)]
    another operation x3 -> x0, other arithmetic: 6.6 us -> none  [the longest x1 4.45 us: body(): jnp.stack(arranged)]
    scatter x4 -> x0, local copies, waits for them, and re-layouts: 6.1 us -> none  [body(): blocked[table].at[:, target]]
    unnamed x14 -> x6, local copies, waits for them, and re-layouts: 7.26 us -> 1.6 us
  transfers between devices with their start and end apart: 1 -> 0, of which waited for: 1 -> 0; matrix products, arithmetic and copies ran while one was open for 5% -> 0% of each run, Pallas kernels for 0% -> 0%
where the time goes in v1:
time: 54.1 us; the launch traced here: 53.9 us
  Pallas kernels  49.9 us (92%)
  other arithmetic  1.76 us (3%)
  local copies, waits for them, and re-layouts  1.6 us (3%)
  between operations  0.69 us (1%)
    pallas_call x1, Pallas kernels, body(): pl.pallas_call(functools.partial(exchange, cfg), out_shape=(jax.ShapeDtyp...  45.7 us
    pallas_call x1, Pallas kernels, body(): pl.pallas_call(functools.partial(update, cfg, dim), out_shape=(jax.ShapeD...  2.93 us
    unnamed x6, local copies, waits for them, and re-layouts  1.6 us
    pallas_call x1, Pallas kernels, body(): pl.pallas_call(functools.partial(pack, cfg), out_shape=jax.ShapeDtypeStru...  1.25 us

profile of v1, /device:TPU:0, one launch (start us, length us, event | category | flops | bytes accessed | tf_op | source)
XLA Modules:
  0.0 53.9 jit_solution(14355578775451369267)
XLA Ops:
  0.6 0.9 %convert_reduce_fusion = s32[2,128]{1,0:T(2,128)S(1)} fusion(s32[2,128]{1,0:T(2,128)} %param.7), kind=kLoop, calls=%fused_computation.3 | loop fusion | flops 98048 | bytes 2048 | tf_op jit(solution)/shard_map/reduce_sum | solution.py:233
  1.6 0.8 %select_reduce_fusion = (s32[2,128]{1,0:T(2,128)S(1)}, s32[2,128]{1,0:T(2,128)S(1)}) fusion(s32[2,128]{1,0:T(2,128)S(1)} %convert_reduce_fusion, s32[2,128]{1,0:T(2,128)} %param.7), kind=kLoop, calls=%fused_computation | loop fusion | flops 163328 | bytes 4096 | tf_op jit(solution)/shard_map/reduce_sum | solution.py:235
  2.4 0.0 copy-start.1
  2.4 1.6 %copy-done.1 = bf16[1,2,32,16384]{3,2,1,0:T(8,128)(2,1)S(1)} copy-done((bf16[1,2,32,16384]{3,2,1,0:T(8,128)(2,1)S(1)}, bf16[1,2,32,16384]{3,2,1,0:T(8,128)(2,1)}, u32[]{:S(2)}) %copy-start.1) | copy-done | bytes 2097176
  4.0 1.2 %pack.1.packed = f32[8,4,32,1024]{3,2,1,0:T(8,128)S(1)} custom-call(s32[2,128]{1,0:T(2,128)S(1)} %get-tuple-element.6.order, bf16[1,2,32,16384]{3,2,1,0:T(8,128)(2,1)S(1)} %copy-done.1), custom_call_target="tpu_custom_call" | custom-call | tf_op jit(solution)/shard_map/pack/pallas_call | solution.py:243
  5.2 0.0 copy-start
  5.3 0.0 copy-start.2
  5.3 45.7 %exchange.1 = (f32[8,32,1024]{2,1,0:T(8,128)S(1)}, f32[8,8,128]{2,1,0:T(8,128)S(1)}) custom-call(f32[8,4,32,1024]{3,2,1,0:T(8,128)S(1)} %pack.1.packed), custom_call_target="tpu_custom_call" | custom-call | tf_op jit(solution)/shard_map/exchange/pallas_call | solution.py:251
  51.0 0.0 copy-done
  51.0 0.0 copy-done.2
  51.0 2.9 %update.1 = (f32[2,32,8192]{2,1,0:T(8,128)}, f32[2,8192]{1,0:T(2,128)}) custom-call(s32[2,128]{1,0:T(2,128)S(1)} %get-tuple-element.7.ids, f32[8,32,1024]{2,1,0:T(8,128)S(1)} %get-tuple-element.4.total, f32[8,8,128]{2,1,0:T(8,128)S(1)} %get-tuple-element.5.squares, f32[2,32,8192]{2,1,0:T(8,128)S(1)} %copy-done, f32[2,8192]{1,0:T(2,128)S(1)} %copy-done.2), custom_call_target="tpu_custom_call" | custom-call | tf_op jit(solution)/shard_map/update/pallas_call | solution.py:272
Async XLA Ops:
  2.4 1.6 %copy-start.1 = (bf16[1,2,32,16384]{3,2,1,0:T(8,128)(2,1)S(1)}, bf16[1,2,32,16384]{3,2,1,0:T(8,128)(2,1)}, u32[]{:S(2)}) copy-start(bf16[1,2,32,16384]{3,2,1,0:T(8,128)(2,1)} %grads.1) | copy-start | bytes 6291460
  5.2 45.8 %copy-start = (f32[2,32,8192]{2,1,0:T(8,128)S(1)}, f32[2,32,8192]{2,1,0:T(8,128)}, u32[]{:S(2)}) copy-start(f32[2,32,8192]{2,1,0:T(8,128)} %tables.1) | copy-start | bytes 6291460
  5.3 45.8 %copy-start.2 = (f32[2,8192]{1,0:T(2,128)S(1)}, f32[2,8192]{1,0:T(2,128)}, u32[]{:S(2)}) copy-start(f32[2,8192]{1,0:T(2,128)} %accumulator.1) | copy-start | bytes 196612

commit v2 on v1

--- a/solution.py
+++ b/solution.py
@@ -10,7 +10,7 @@
 
 BLOCK = 128
 MESH = pl.DeviceIdType.MESH
-AHEAD = 2
+GROUP = 16
 
 
 def layout(mesh, shape, n_slab):
@@ -20,13 +20,26 @@
         inner -= 1
     ntab, width, _ = shape
     per = n_slab // BLOCK // reps
-    group = math.gcd(per, 8)
+    group = math.gcd(per, GROUP)
     return dict(reps=reps, cols=cols, inner=inner, outer=reps // inner, ntab=ntab,
                 width=width, per=per, group=group, pieces=per // group)
 
 
-def pack(cfg, order, grads, packed):
+def pack(cfg, block_ids, grads, packed, ids_out, order_vec, order, order_sem):
     reps, per, group, pieces = cfg["reps"], cfg["per"], cfg["group"], cfg["pieces"]
+    ntab, nblk = block_ids.shape
+    lane = lax.broadcasted_iota(jnp.int32, (nblk, nblk), 1).astype(jnp.float32)
+    slot = lax.broadcasted_iota(jnp.int32, (nblk, nblk), 0).astype(jnp.float32)
+    for t in range(ntab):
+        across = jnp.broadcast_to(block_ids[pl.ds(t, 1), :].astype(jnp.float32), (nblk, nblk))
+        down = across.T
+        place = jnp.sum(jnp.where(across < down, 1.0, 0.0), axis=1, keepdims=True)
+        hit = place == lane
+        order_vec[pl.ds(t, 1), :] = jnp.sum(jnp.where(hit, slot, 0.0), axis=0, keepdims=True).astype(jnp.int32)
+        ids_out[pl.ds(t, 1), :] = jnp.sum(jnp.where(hit, down, 0.0), axis=0, keepdims=True).astype(jnp.int32)
+    to_scalar = pltpu.make_async_copy(order_vec, order, order_sem)
+    to_scalar.start()
+    to_scalar.wait()
 
     def piece(t, g):
         for owner in range(reps):
@@ -35,7 +48,7 @@
                 lanes = pl.ds(pl.multiple_of(at * BLOCK, BLOCK), BLOCK)
                 packed[t * pieces + g, owner, :, pl.ds(i * BLOCK, BLOCK)] = grads[0, t, :, lanes].astype(jnp.float32)
 
-    for t in range(cfg["ntab"]):
+    for t in range(ntab):
         lax.fori_loop(0, pieces, lambda g, n, t=t: (piece(t, g), n)[1], 0)
 
 
@@ -89,11 +102,15 @@
             sq_all.at[c, my_col], sq_all.at[c, my_col], s3.at[c, f - 1], r3.at[c, f - 1],
             device_id={"col": lax.rem(my_col + f, cols)}, device_id_type=MESH)
 
-    def send(c):
+    def send_far(c):
         nf, ns = axes(c)
-        for s in [*range(1, ns), 0]:
+        for s in range(1, ns):
             for f in range(1, nf):
                 first_copy(c, f, s).start()
+
+    def send_near(c):
+        for f in range(1, axes(c)[0]):
+            first_copy(c, f, 0).start()
 
     def relay(c):
         nf, ns = axes(c)
@@ -155,13 +172,15 @@
                     fn(c)
 
     greeted = inner - 1 + outer - 1 + cols - 1
-    for k in range(steps + AHEAD + 4):
-        if k == 0:
-            pl.semaphore_wait(barrier, greeted)
-        at(k, [send])
-        at(k - AHEAD + 1, [relay, send_relay])
-        at(k - AHEAD - 0, [finish, send_squares])
-        at(k - AHEAD - 1, [gather_squares])
+    pl.semaphore_wait(barrier, greeted)
+    for k in range(steps):
+        at(k, [send_far])
+    for k in range(steps):
+        at(k, [send_near])
+    for k in range(steps + 2):
+        at(k, [relay, send_relay])
+        at(k - 1, [finish, send_squares])
+        at(k - 2, [gather_squares])
 
     for c in range(chunks):
         nf, ns = axes(c)
@@ -230,24 +249,25 @@
     nslab = replica_grads.shape[3]
     nblk = nslab // BLOCK
 
-    place = jnp.sum((block_ids[:, :, None] > block_ids[:, None, :]).astype(jnp.int32), axis=2)
-    hit = place[:, None, :] == jnp.arange(nblk, dtype=jnp.int32)[None, :, None]
-    order = jnp.sum(jnp.where(hit, jnp.arange(nblk, dtype=jnp.int32)[None, None, :], 0), axis=2)
-    ids = jnp.sum(jnp.where(hit, block_ids[:, None, :], 0), axis=2)
-
     anyspace = pl.BlockSpec(memory_space=pl.ANY)
     vmem = pl.BlockSpec(memory_space=pltpu.VMEM)
     smem = pl.BlockSpec(memory_space=pltpu.SMEM)
     f32 = jnp.float32
     dma = pltpu.SemaphoreType.DMA
-    packed = pl.pallas_call(
+    packed, ids = pl.pallas_call(
         functools.partial(pack, cfg),
-        out_shape=jax.ShapeDtypeStruct((chunks, cfg["reps"], width, span), f32),
-        in_specs=[smem, vmem],
-        out_specs=vmem,
-        compiler_params=pltpu.CompilerParams(vmem_limit_bytes=12 * 2**20),
+        out_shape=(jax.ShapeDtypeStruct((chunks, cfg["reps"], width, span), f32),
+                   jax.ShapeDtypeStruct(block_ids.shape, jnp.int32)),
+        in_specs=[vmem, vmem],
+        out_specs=(vmem, vmem),
+        scratch_shapes=[
+            pltpu.VMEM((ntab, nblk), jnp.int32),
+            pltpu.SMEM((ntab, nblk), jnp.int32),
+            dma(()),
+        ],
+        compiler_params=pltpu.CompilerParams(vmem_limit_bytes=16 * 2**20),
         name="pack",
-    )(order, replica_grads)
+    )(block_ids, replica_grads)
     total, squares = pl.pallas_call(
         functools.partial(exchange, cfg),
         out_shape=(jax.ShapeDtypeStruct((chunks, width, span), f32),

time: 54.1 us -> 52.8 us (0.976)
  other arithmetic: 1.76 us -> 0 us
  local copies, waits for them, and re-layouts: 1.6 us -> 2.28 us
    reduce_sum x2 -> x0, other arithmetic: 1.76 us -> none  [the longest x1 0.93 us: body(): jnp.sum((block_ids[:, :, None] > block_ids[:, None, :]).astype(jnp.int32)...]
    unnamed x6 -> x8, local copies, waits for them, and re-layouts: 1.6 us -> 2.28 us
where the time goes in v2:
time: 52.8 us; the launch traced here: 52.6 us
  Pallas kernels  49.7 us (94%)
  local copies, waits for them, and re-layouts  2.28 us (4%)
  between operations  0.69 us (1%)
    pallas_call x1, Pallas kernels, body(): pl.pallas_call(functools.partial(exchange, cfg), out_shape=(jax.ShapeDtyp...  45.3 us
    pallas_call x1, Pallas kernels, body(): pl.pallas_call(functools.partial(update, cfg, dim), out_shape=(jax.ShapeD...  2.93 us
    unnamed x8, local copies, waits for them, and re-layouts  2.28 us
    pallas_call x1, Pallas kernels, body(): pl.pallas_call(functools.partial(pack, cfg), out_shape=(jax.ShapeDtypeStr...  1.42 us

profile of v2, /device:TPU:0, one launch (start us, length us, event | category | flops | bytes accessed | tf_op | source)
XLA Modules:
  0.0 52.6 jit_solution(746325786938613238)
XLA Ops:
  0.6 0.0 copy-start.1
  0.6 1.6 %copy-done.1 = bf16[1,2,32,16384]{3,2,1,0:T(8,128)(2,1)S(1)} copy-done((bf16[1,2,32,16384]{3,2,1,0:T(8,128)(2,1)S(1)}, bf16[1,2,32,16384]{3,2,1,0:T(8,128)(2,1)}, u32[]{:S(2)}) %copy-start.1) | copy-done | bytes 2097176
  2.2 0.0 copy-start.3
  2.2 0.7 %copy-done.3 = s32[2,128]{1,0:T(2,128)S(1)} copy-done((s32[2,128]{1,0:T(2,128)S(1)}, s32[2,128]{1,0:T(2,128)}, u32[]{:S(2)}) %copy-start.3) | copy-done | bytes 1048
  2.9 1.4 %pack.1 = (f32[4,4,32,2048]{3,2,1,0:T(8,128)S(1)}, s32[2,128]{1,0:T(2,128)S(1)}) custom-call(s32[2,128]{1,0:T(2,128)S(1)} %copy-done.3, bf16[1,2,32,16384]{3,2,1,0:T(8,128)(2,1)S(1)} %copy-done.1), custom_call_target="tpu_custom_call" | custom-call | tf_op jit(solution)/shard_map/pack/pallas_call | solution.py:257
  4.3 0.0 copy-start
  4.3 0.0 copy-start.2
  4.4 45.3 %exchange.1 = (f32[4,32,2048]{2,1,0:T(8,128)S(1)}, f32[4,16,128]{2,1,0:T(8,128)S(1)}) custom-call(f32[4,4,32,2048]{3,2,1,0:T(8,128)S(1)} %get-tuple-element.7.packed), custom_call_target="tpu_custom_call" | custom-call | tf_op jit(solution)/shard_map/exchange/pallas_call | solution.py:271
  49.7 0.0 copy-done
  49.7 0.0 copy-done.2
  49.7 2.9 %update.1 = (f32[2,32,8192]{2,1,0:T(8,128)}, f32[2,8192]{1,0:T(2,128)}) custom-call(s32[2,128]{1,0:T(2,128)S(1)} %get-tuple-element.6.ids, f32[4,32,2048]{2,1,0:T(8,128)S(1)} %get-tuple-element.8.total, f32[4,16,128]{2,1,0:T(8,128)S(1)} %get-tuple-element.9.squares, f32[2,32,8192]{2,1,0:T(8,128)S(1)} %copy-done, f32[2,8192]{1,0:T(2,128)S(1)} %copy-done.2), custom_call_target="tpu_custom_call" | custom-call | tf_op jit(solution)/shard_map/update/pallas_call | solution.py:292
Async XLA Ops:
  0.6 1.6 %copy-start.1 = (bf16[1,2,32,16384]{3,2,1,0:T(8,128)(2,1)S(1)}, bf16[1,2,32,16384]{3,2,1,0:T(8,128)(2,1)}, u32[]{:S(2)}) copy-start(bf16[1,2,32,16384]{3,2,1,0:T(8,128)(2,1)} %grads.1) | copy-start | bytes 6291460
  2.2 0.7 %copy-start.3 = (s32[2,128]{1,0:T(2,128)S(1)}, s32[2,128]{1,0:T(2,128)}, u32[]{:S(2)}) copy-start(s32[2,128]{1,0:T(2,128)} %block_ids.1) | copy-start | bytes 3076
  4.3 45.3 %copy-start = (f32[2,32,8192]{2,1,0:T(8,128)S(1)}, f32[2,32,8192]{2,1,0:T(8,128)}, u32[]{:S(2)}) copy-start(f32[2,32,8192]{2,1,0:T(8,128)} %tables.1) | copy-start | bytes 6291460
  4.3 45.3 %copy-start.2 = (f32[2,8192]{1,0:T(2,128)S(1)}, f32[2,8192]{1,0:T(2,128)}, u32[]{:S(2)}) copy-start(f32[2,8192]{1,0:T(2,128)} %accumulator.1) | copy-start | bytes 196612
